TPU v7x, 32 devices: a whole 2x2x4 slice. The times are simulated.
32 devices in a mesh: gx: 2 (over y), gy: 4 (over z), gz: 4 (over x, core).
Axes of the slice: x: 2, y: 2, z: 4, core: 2. Of those that a mesh axis runs over, the one named last changes fastest.
Arguments:
- forcing: float32 [3, 16, 64, 512], P(None, 'gx', 'gy', 'gz'), may hold values from -8 to 8
- viscosity: float32 [16, 64, 512], P('gx', 'gy', 'gz'), may hold values from 0.001 to 1000
Outputs:
- solution: float32 [3, 16, 64, 512], P(None, 'gx', 'gy', 'gz')
- residual: float32 [3, 16, 64, 512], P(None, 'gx', 'gy', 'gz')
All inputs are finite; a program needn't handle non-finite values.
Results may differ from a plain program's by a relative error of at most 0.00017.
Values sent between devices are 32-bit elements; how exact they have to be, the bound alone decides.
A program may use at most 64 MiB of HBM per device.

v0:
```python
import jax
import jax.numpy as jnp
from jax import lax
from jax.sharding import PartitionSpec as P

ITERS = 3
CSWEEPS = 4
reaction = 1.0
relaxation = 2.0 / 3.0
neighbours = ((1, 0, 0), (-1, 0, 0), (0, 1, 0), (0, -1, 0), (0, 0, 1), (0, 0, -1))


def with_halo(x, sides, width):
    for axis, dim in sides:
        count, length = (lax.axis_size(axis), x.shape[dim])
        up = [(i, (i + 1) % count) for i in range(count - 1)]
        down = [(j, i) for i, j in up]
        last = lax.slice_in_dim(x, length - width, length, axis=dim)
        initial = lax.slice_in_dim(x, 0, width, axis=dim)
        before = lax.ppermute(last, axis, up)
        after = lax.ppermute(initial, axis, down)
        x = jnp.concatenate([before, x, after], axis=dim)
    return x


def window(padded, offset, extent):
    return padded[
        ...,
        1 + offset[0] : 1 + offset[0] + extent[0],
        1 + offset[1] : 1 + offset[1] + extent[1],
        1 + offset[2] : 1 + offset[2] + extent[2],
    ]


def viscous(values, padded_values, viscosity, padded_visc, mass_term, face_term):
    extent = viscosity.shape
    summed = mass_term * values
    for offset in neighbours:
        beside = window(padded_visc, offset, extent)
        across = window(padded_values, offset, extent)
        summed = summed + face_term * (viscosity + beside) * (values - across)
    return summed


def diagonal_of(viscosity, padded_visc, mass_term, face_term):
    summed = jnp.full(viscosity.shape, mass_term, jnp.float32)
    for offset in neighbours:
        summed = summed + face_term * (viscosity + window(padded_visc, offset, viscosity.shape))
    return summed


def restrict(values):
    extent = values.shape
    return values.reshape(extent[0], extent[1] // 2, 2, extent[2] // 2, 2, extent[3] // 2, 2).sum(
        axis=(2, 4, 6)
    )


def prolong(values):
    return jnp.repeat(jnp.repeat(jnp.repeat(values, 2, axis=1), 2, axis=2), 2, axis=3)


def coarsen(viscosity):
    extent = viscosity.shape
    return viscosity.reshape(extent[0] // 2, 2, extent[1] // 2, 2, extent[2] // 2, 2).mean(
        axis=(1, 3, 5)
    )


def sweeps(coarse_rhs, diagonal, applier):
    correction = relaxation * coarse_rhs / diagonal
    for counter in range(CSWEEPS - 1):
        correction = correction + relaxation * (coarse_rhs - applier(correction)) / diagonal
    return correction


def precond_product(residual, precond):
    return lax.psum(jnp.sum(residual * precond), ("gx", "gy", "gz"))


def shards(forcing, viscosity):
    padded_visc = with_halo(viscosity, (("gx", 0), ("gy", 1), ("gz", 2)), 1)
    fine_diag = diagonal_of(viscosity, padded_visc, reaction, 0.5)
    coarse_visc = coarsen(viscosity)

    def fine_apply(values):
        padded = with_halo(values, (("gx", 1), ("gy", 2), ("gz", 3)), 1)
        return viscous(values, padded, viscosity, padded_visc, reaction, 0.5)

    group_visc = lax.all_gather(coarse_visc, "gz", axis=2, tiled=True)
    group_pad = with_halo(group_visc, (("gx", 0), ("gy", 1)), 1)
    group_pad = jnp.pad(group_pad, ((0, 0), (0, 0), (1, 1)))
    group_diag = diagonal_of(group_visc, group_pad, 8.0 * reaction, 2.0)
    depth_local = coarse_visc.shape[2]
    offset_z = lax.axis_index("gz") * depth_local

    def group_apply(values):
        padded = with_halo(values, (("gx", 1), ("gy", 2)), 1)
        padded = jnp.pad(padded, ((0, 0), (0, 0), (0, 0), (1, 1)))
        return viscous(values, padded, group_visc, group_pad, 8.0 * reaction, 2.0)

    def coarse_solve(coarse_rhs):
        whole_line = lax.all_gather(coarse_rhs, "gz", axis=3, tiled=True)
        correction = sweeps(whole_line, group_diag, group_apply)
        return lax.dynamic_slice_in_dim(correction, offset_z, depth_local, 3)

    def precondition(residual):
        smoothed = relaxation * residual / fine_diag
        defect = residual - fine_apply(smoothed)
        correction = coarse_solve(restrict(defect))
        smoothed = smoothed + prolong(correction)
        return smoothed + relaxation * (residual - fine_apply(smoothed)) / fine_diag

    solution = jnp.zeros_like(forcing)
    residual = forcing
    precond = precondition(residual)
    product = precond_product(residual, precond)
    direction = precond
    for iteration in range(ITERS):
        applied = fine_apply(direction)
        alpha_step = product / lax.psum(jnp.sum(direction * applied), ("gx", "gy", "gz"))
        solution = solution + alpha_step * direction
        residual = residual - alpha_step * applied
        if iteration + 1 < ITERS:
            precond = precondition(residual)
            product_next = precond_product(residual, precond)
            direction = precond + product_next / product * direction
            product = product_next
    return (solution, residual)


def solution(mesh):
    return jax.shard_map(
        shards,
        mesh=mesh,
        in_specs=(P(None, "gx", "gy", "gz"), P("gx", "gy", "gz")),
        out_specs=(P(None, "gx", "gy", "gz"), P(None, "gx", "gy", "gz")),
        check_vma=False,
    )
```

profile of v0, /device:TPU:0, one launch (start us, length us, event | category | flops | bytes accessed | tf_op | source)
XLA Modules:
  0.0 754.0 jit_solution(5678509347087031177)
XLA Ops:
  1.3 4.9 collective-permute-start.1
  7.5 6.3 reshape.58
  21.4 7.2 all_gather.13
  32.5 4.5 collective-permute-start.13
  38.6 4.5 collective-permute-start.7
  44.5 4.5 collective-permute-start.15
  50.4 4.5 collective-permute-start.9
  56.4 4.1 collective-permute-done.8
  66.7 13.9 %reshape.57 = f32[3,4,2,8,2,64,2]{6,5,4,3,2,1,0:T(8,128)} reshape(f32[3,8,16,128]{3,2,1,0:T(8,128)S(1)} %fusion.162) | data formatting | bytes 393216 | tf_op jit(solution)/shard_map/reshape | solution.py:54
  80.7 5.5 reduce_sum.90
  86.4 19.3 %all_gather.12 = f32[3,4,8,256]{2,1,0,3:T(4,128)S(1)} all-gather(f32[3,4,8,64]{2,1,0,3:T(4,128)S(1)} %copy.996), channel_id=1, replica_groups=mesh['gx'=2,'gy'=4,'gz'=4] {'gz'}, dimensions={3}, use_global_device_ids=true | all-gather | bytes 122880 | tf_op jit(solution)/shard_map/all_gather | solution.py:103
  106.3 4.5 collective-permute-start.17
  112.4 4.2 collective-permute-done.16
  121.6 4.2 collective-permute-done.18
  129.4 4.2 collective-permute-done.20
  138.6 4.2 collective-permute-done.22
  146.4 4.2 collective-permute-done.24
  154.0 4.2 collective-permute-done.26
  165.0 4.2 collective-permute-done.28
  172.6 4.2 collective-permute-done.30
  186.2 4.2 collective-permute-done.34
  193.8 4.2 collective-permute-done.36
  204.8 46.7 %all-reduce.10 = (f32[]{:T(128)}, f32[]{:T(128)}) all-reduce(f32[]{:T(128)} %get-tuple-element.13, f32[]{:T(128)} %get-tuple-element.12), channel_id=1, replica_groups=mesh['gx'=2,'gy'=4,'gz'=4] {'gx','gy','gz'}, use_global_device_ids=true, to_apply=%region_3.4 | all-reduce | flops 2 | bytes 16 | tf_op jit(solution)/shard_map/psum | solution.py:78
  252.9 4.4 collective-permute-start.41
  258.7 4.2 collective-permute-done.40
  263.0 3.8 collective-permute-start.43
  268.2 4.2 collective-permute-done.42
  278.6 13.9 %reshape.62 = f32[3,4,2,8,2,64,2]{6,5,4,3,2,1,0:T(8,128)} reshape(f32[3,8,16,128]{3,2,1,0:T(8,128)S(1)} %fusion.103) | data formatting | bytes 393216 | tf_op jit(solution)/shard_map/reshape | solution.py:54
  292.6 5.5 reduce_sum.94
  298.3 18.5 %all_gather.14 = f32[3,4,8,256]{2,1,0,3:T(4,128)S(1)} all-gather(f32[3,4,8,64]{2,1,0,3:T(4,128)S(1)} %copy.1016), channel_id=1, replica_groups=mesh['gx'=2,'gy'=4,'gz'=4] {'gz'}, dimensions={3}, use_global_device_ids=true | all-gather | bytes 122880 | tf_op jit(solution)/shard_map/all_gather | solution.py:103
  320.5 4.2 collective-permute-done.46
  328.8 4.2 collective-permute-done.48
  336.6 4.2 collective-permute-done.50
  344.2 4.2 collective-permute-done.52
  352.0 4.2 collective-permute-done.54
  359.7 4.2 collective-permute-done.56
  370.7 4.2 collective-permute-done.58
  378.3 4.2 collective-permute-done.60
  389.3 41.5 %psum.44 = f32[]{:T(128)} all-reduce(f32[]{:T(128)} %get-tuple-element.24), channel_id=1, replica_groups=mesh['gx'=2,'gy'=4,'gz'=4] {'gx','gy','gz'}, use_global_device_ids=true, to_apply=%region_8.9 | all-reduce | flops 1 | bytes 8 | tf_op jit(solution)/shard_map/psum | solution.py:78
  432.1 4.4 collective-permute-start.65
  438.1 4.2 collective-permute-done.64
  442.3 3.8 collective-permute-start.67
  447.6 4.2 collective-permute-done.66
  458.5 43.7 %psum.45 = f32[]{:T(128)} all-reduce(f32[]{:T(128)} %get-tuple-element.22), channel_id=1, replica_groups=mesh['gx'=2,'gy'=4,'gz'=4] {'gx','gy','gz'}, use_global_device_ids=true, to_apply=%region_10.11 | all-reduce | flops 1 | bytes 8 | tf_op jit(solution)/shard_map/psum | solution.py:121
  503.6 4.4 collective-permute-start.71
  509.5 4.2 collective-permute-done.70
  518.5 4.1 collective-permute-done.72
  528.8 13.9 %reshape.66 = f32[3,4,2,8,2,64,2]{6,5,4,3,2,1,0:T(8,128)} reshape(f32[3,8,16,128]{3,2,1,0:T(8,128)S(1)} %fusion.44) | data formatting | bytes 393216 | tf_op jit(solution)/shard_map/reshape | solution.py:54
  542.8 5.5 reduce_sum.97
  548.5 18.5 %all_gather.15 = f32[3,4,8,256]{2,1,0,3:T(4,128)S(1)} all-gather(f32[3,4,8,64]{2,1,0,3:T(4,128)S(1)} %copy.1024), channel_id=1, replica_groups=mesh['gx'=2,'gy'=4,'gz'=4] {'gz'}, dimensions={3}, use_global_device_ids=true | all-gather | bytes 122880 | tf_op jit(solution)/shard_map/all_gather | solution.py:103
  570.7 4.2 collective-permute-done.76
  579.0 4.2 collective-permute-done.78
  586.8 4.2 collective-permute-done.80
  595.1 4.2 collective-permute-done.82
  602.9 4.2 collective-permute-done.84
  610.5 4.2 collective-permute-done.86
  619.7 4.2 collective-permute-done.88
  627.3 4.2 collective-permute-done.90
  638.3 41.5 %psum.46 = f32[]{:T(128)} all-reduce(f32[]{:T(128)} %get-tuple-element.18), channel_id=1, replica_groups=mesh['gx'=2,'gy'=4,'gz'=4] {'gx','gy','gz'}, use_global_device_ids=true, to_apply=%region_13.14 | all-reduce | flops 1 | bytes 8 | tf_op jit(solution)/shard_map/psum | solution.py:78
  681.1 4.4 collective-permute-start.95
  687.0 4.2 collective-permute-done.94
  691.3 3.8 collective-permute-start.97
  696.5 4.2 collective-permute-done.96
  707.5 43.7 %psum.47 = f32[]{:T(128)} all-reduce(f32[]{:T(128)} %get-tuple-element.16), channel_id=1, replica_groups=mesh['gx'=2,'gy'=4,'gz'=4] {'gx','gy','gz'}, use_global_device_ids=true, to_apply=%region_15.16 | all-reduce | flops 1 | bytes 8 | tf_op jit(solution)/shard_map/psum | solution.py:121
  (301 shorter events, 195.9 us)
Async XLA Ops:
  1.3 15.2 %collective-permute-start.1 = (f32[1,16,128]{2,1,0:T(8,128)S(1)}, f32[1,16,128]{2,1,0:T(8,128)S(1)}, u32[]{:S(2)}, u32[]{:S(2)}) collective-permute-start(f32[1,16,128]{2,1,0:T(8,128)S(1)} %get-tuple-element.143), channel_id=1, source_target_pairs={{0,16},{1,17},{2,18},{3,19},{4,20},{5,21},{6,22},{7,23},{8,24},{9,... | collective-permute-start | bytes 24584 | tf_op jit(solution)/shard_map/ppermute | solution.py:20
  6.2 10.4 %collective-permute-start = (f32[1,16,128]{2,1,0:T(8,128)S(1)}, f32[1,16,128]{2,1,0:T(8,128)S(1)}, u32[]{:S(2)}, u32[]{:S(2)}) collective-permute-start(f32[1,16,128]{2,1,0:T(8,128)S(1)} %get-tuple-element.144), channel_id=1, source_target_pairs={{16,0},{17,1},{18,2},{19,3},{20,4},{21,5},{22,6},{23,7},{24,8},{25... | collective-permute-start | bytes 24584 | tf_op jit(solution)/shard_map/ppermute | solution.py:21
  16.6 12.1 %collective-permute-start.3 = (f32[10,1,128]{2,1,0:T(1,128)S(1)}, f32[10,1,128]{2,1,0:T(1,128)S(1)}, u32[]{:S(2)}, u32[]{:S(2)}) collective-permute-start(f32[10,1,128]{2,1,0:T(1,128)S(1)} %get-tuple-element.141), channel_id=1, source_target_pairs={{0,4},{4,8},{8,12},{1,5},{5,9},{9,13},{2,6},{6,10},{10,14},{3,7},{... | collective-permute-start | bytes 15368 | tf_op jit(solution)/shard_map/ppermute | solution.py:20
  20.1 8.7 %collective-permute-start.2 = (f32[10,1,128]{2,1,0:T(1,128)S(1)}, f32[10,1,128]{2,1,0:T(1,128)S(1)}, u32[]{:S(2)}, u32[]{:S(2)}) collective-permute-start(f32[10,1,128]{2,1,0:T(1,128)S(1)} %get-tuple-element.142), channel_id=1, source_target_pairs={{4,0},{8,4},{12,8},{5,1},{9,5},{13,9},{6,2},{10,6},{14,10},{7,3},{... | collective-permute-start | bytes 15368 | tf_op jit(solution)/shard_map/ppermute | solution.py:21
  28.9 9.4 %collective-permute-start.5 = (f32[10,18,1]{2,1,0:T(8,128)S(1)}, f32[10,18,1]{2,1,0:T(8,128)S(1)}, u32[]{:S(2)}, u32[]{:S(2)}) collective-permute-start(f32[10,18,1]{2,1,0:T(8,128)S(1)} %get-tuple-element.121), channel_id=1, source_target_pairs={{0,1},{1,2},{2,3},{4,5},{5,6},{6,7},{8,9},{9,10},{10,11},{12,13},{... | collective-permute-start | bytes 2168 | tf_op jit(solution)/shard_map/ppermute | solution.py:20
  31.2 7.2 collective-permute-start.4
  32.5 11.9 %collective-permute-start.13 = (f32[1,8,256]{2,1,0:T(8,128)S(1)}, f32[1,8,256]{2,1,0:T(8,128)S(1)}, u32[]{:S(2)}, u32[]{:S(2)}) collective-permute-start(f32[1,8,256]{2,1,0:T(8,128)S(1)} %get-tuple-element.147), channel_id=1, source_target_pairs={{0,16},{1,17},{2,18},{3,19},{4,20},{5,21},{6,22},{7,23},{8,24},{9,... | collective-permute-start | bytes 24584 | tf_op jit(solution)/shard_map/ppermute | solution.py:20
  37.0 7.4 collective-permute-start.12
  38.6 11.7 %collective-permute-start.7 = (f32[3,1,16,128]{3,2,1,0:T(8,128)S(1)}, f32[3,1,16,128]{3,2,1,0:T(8,128)S(1)}, u32[]{:S(2)}, u32[]{:S(2)}) collective-permute-start(f32[3,1,16,128]{3,2,1,0:T(8,128)S(1)} %get-tuple-element.101), channel_id=1, source_target_pairs={{0,16},{1,17},{2,18},{3,19},{4,20},{5,21},{6,22},{7,23},{8,24},{9,... | collective-permute-start | bytes 73736 | tf_op jit(solution)/shard_map/ppermute | solution.py:20
  43.1 7.2 collective-permute-start.6
  44.5 11.8 %collective-permute-start.15 = (f32[6,1,256]{2,1,0:T(1,128)S(1)}, f32[6,1,256]{2,1,0:T(1,128)S(1)}, u32[]{:S(2)}, u32[]{:S(2)}) collective-permute-start(f32[6,1,256]{2,1,0:T(1,128)S(1)} %get-tuple-element.145), channel_id=1, source_target_pairs={{0,4},{4,8},{8,12},{1,5},{5,9},{9,13},{2,6},{6,10},{10,14},{3,7},{... | collective-permute-start | bytes 18440 | tf_op jit(solution)/shard_map/ppermute | solution.py:20
  49.0 7.2 collective-permute-start.14
  50.4 6.0 collective-permute-start.9
  54.9 5.6 collective-permute-start.8
  60.8 4.5 collective-permute-start.10
  106.3 6.1 collective-permute-start.17
  110.9 5.7 collective-permute-start.16
  116.7 4.9 collective-permute-start.19
  120.2 5.7 collective-permute-start.18
  127.9 5.7 collective-permute-start.20
  133.7 4.9 collective-permute-start.23
  137.1 5.7 collective-permute-start.22
  144.9 5.7 collective-permute-start.24
  152.6 5.7 collective-permute-start.26
  163.5 5.7 collective-permute-start.28
  171.2 5.6 collective-permute-start.30
  177.1 4.4 collective-permute-start.32
  184.7 5.7 collective-permute-start.34
  192.4 5.6 collective-permute-start.36
  198.2 4.5 collective-permute-start.38
  252.9 5.9 collective-permute-start.41
  257.2 5.7 collective-permute-start.40
  263.0 5.3 collective-permute-start.43
  266.8 5.6 collective-permute-start.42
  272.7 4.4 collective-permute-start.44
  319.0 5.7 collective-permute-start.46
  327.4 5.7 collective-permute-start.48
  335.1 5.7 collective-permute-start.50
  342.8 5.7 collective-permute-start.52
  350.5 5.7 collective-permute-start.54
  358.2 5.7 collective-permute-start.56
  369.2 5.7 collective-permute-start.58
  376.9 5.6 collective-permute-start.60
  432.1 5.9 collective-permute-start.65
  436.6 5.7 collective-permute-start.64
  442.3 5.3 collective-permute-start.67
  446.2 5.6 collective-permute-start.66
  503.6 5.9 collective-permute-start.71
  508.0 5.7 collective-permute-start.70
  513.8 4.8 collective-permute-start.73
  517.0 5.6 collective-permute-start.72
  569.2 5.7 collective-permute-start.76
  577.5 5.7 collective-permute-start.78
  585.3 5.7 collective-permute-start.80
  593.6 5.7 collective-permute-start.82
  601.4 5.7 collective-permute-start.84
  609.0 5.7 collective-permute-start.86
  618.2 5.7 collective-permute-start.88
  625.8 5.6 collective-permute-start.90
  681.1 5.9 collective-permute-start.95
  685.5 5.7 collective-permute-start.94
  691.3 5.3 collective-permute-start.97
  695.1 5.6 collective-permute-start.96
  701.0 4.4 collective-permute-start.98
  (40 other events, 204.1 us)
where the time goes:
time: 757 us; the launch traced here: 754 us
  blocking collectives  281 us (37%)
  starting transfers between devices  208 us (27%)
  waiting for transfers between devices  164 us (22%)
  local copies, waits for them, and re-layouts  60.2 us (8%)
  other arithmetic  32.7 us (4%)
  between operations  8.96 us (1%)
    ppermute x50, waiting for transfers between devices, with_halo(): after = lax.ppermute(initial, axis, down)  147 us
    ppermute x50, starting transfers between devices, with_halo(): before = lax.ppermute(last, axis, up)  143 us
    psum x3, blocking collectives, precond_product(): return lax.psum(jnp.sum(residual * precond), ('gx', 'gy', 'gz'))  130 us
    psum x2, blocking collectives, shards(): lax.psum(jnp.sum(direction * applied), ('gx', 'gy', 'gz'))  87.4 us
    ppermute x50, starting transfers between devices, with_halo(): after = lax.ppermute(initial, axis, down)  64.8 us
    all_gather x3, blocking collectives, coarse_solve(): whole_line = lax.all_gather(coarse_rhs, 'gz', axis=3, tiled=True)  56.3 us
    reshape x3, local copies, waits for them, and re-layouts, restrict(): values.reshape(extent[0], extent[1] // 2, 2, extent[2] // 2, 2, extent[3]...  41.8 us
    ppermute x50, waiting for transfers between devices, with_halo(): before = lax.ppermute(last, axis, up)  16.6 us
  transfers between devices with their start and end apart: 100, of which 77 were waited for; matrix products, arithmetic and copies ran while one was open for 1% of the time, Pallas kernels for 0%

commit v1 on v0

--- a/solution.py
+++ b/solution.py
@@ -100,7 +100,8 @@
         return viscous(values, padded, group_visc, group_pad, 8.0 * reaction, 2.0)
 
     def coarse_solve(coarse_rhs):
-        whole_line = lax.all_gather(coarse_rhs, "gz", axis=3, tiled=True)
+        parts = lax.all_gather(coarse_rhs, "gz", axis=0, tiled=False)
+        whole_line = jnp.concatenate(parts, axis=3)
         correction = sweeps(whole_line, group_diag, group_apply)
         return lax.dynamic_slice_in_dim(correction, offset_z, depth_local, 3)
 

time: 757 us -> 738 us (0.975)
  blocking collectives: 281 us -> 261 us
    all_gather x3, blocking collectives: 56.3 us -> 33.9 us  [coarse_solve(): parts = lax.all_gather(coarse_rhs, 'gz', axis=0, tiled=False)]
where the time goes in v1:
time: 738 us; the launch traced here: 735 us
  blocking collectives  261 us (35%)
  starting transfers between devices  209 us (28%)
  waiting for transfers between devices  164 us (22%)
  local copies, waits for them, and re-layouts  58.7 us (8%)
  other arithmetic  33.6 us (5%)
  between operations  8.84 us (1%)
    ppermute x50, waiting for transfers between devices, with_halo(): after = lax.ppermute(initial, axis, down)  147 us
    ppermute x50, starting transfers between devices, with_halo(): before = lax.ppermute(last, axis, up)  144 us
    psum x3, blocking collectives, precond_product(): return lax.psum(jnp.sum(residual * precond), ('gx', 'gy', 'gz'))  132 us
    psum x2, blocking collectives, shards(): lax.psum(jnp.sum(direction * applied), ('gx', 'gy', 'gz'))  87.4 us
    ppermute x50, starting transfers between devices, with_halo(): after = lax.ppermute(initial, axis, down)  64.9 us
    reshape x3, local copies, waits for them, and re-layouts, restrict(): values.reshape(extent[0], extent[1] // 2, 2, extent[2] // 2, 2, extent[3]...  41.8 us
    all_gather x3, blocking collectives, coarse_solve(): parts = lax.all_gather(coarse_rhs, 'gz', axis=0, tiled=False)  33.9 us
    ppermute x50, waiting for transfers between devices, with_halo(): before = lax.ppermute(last, axis, up)  16.6 us
  transfers between devices with their start and end apart: 100, of which 77 were waited for; matrix products, arithmetic and copies ran while one was open for 1% of the time, Pallas kernels for 0%

profile of v1, /device:TPU:0, one launch (start us, length us, event | category | flops | bytes accessed | tf_op | source)
XLA Modules:
  0.0 734.8 jit_solution(9551145757115760928)
XLA Ops:
  1.3 4.9 collective-permute-start.1
  7.7 6.3 reshape.78
  21.6 7.2 all_gather.23
  32.6 4.5 collective-permute-start.13
  38.7 4.5 collective-permute-start.7
  44.6 4.5 collective-permute-start.15
  50.5 4.5 collective-permute-start.9
  56.5 4.1 collective-permute-done.8
  66.9 13.9 %reshape.75 = f32[3,4,2,8,2,64,2]{6,5,4,3,2,1,0:T(8,128)} reshape(f32[3,8,16,128]{3,2,1,0:T(8,128)S(1)} %fusion.162) | data formatting | bytes 393216 | tf_op jit(solution)/shard_map/reshape | solution.py:54
  80.8 5.5 reduce_sum.90
  86.3 11.9 %all-gather = f32[12,4,8,64]{3,2,1,0:T(8,128)S(1)} all-gather(f32[3,4,8,64]{3,2,1,0:T(8,128)S(1)} %reduce_sum.90), channel_id=2, replica_groups=mesh['gx'=2,'gy'=4,'gz'=4] {'gz'}, dimensions={0}, use_global_device_ids=true | all-gather | bytes 122880 | tf_op jit(solution)/shard_map/all_gather | solution.py:103
  98.5 4.5 collective-permute-start.17
  104.6 4.2 collective-permute-done.16
  113.7 4.2 collective-permute-done.18
  121.6 4.2 collective-permute-done.20
  130.7 4.2 collective-permute-done.22
  138.5 4.2 collective-permute-done.24
  146.2 4.2 collective-permute-done.26
  157.2 4.2 collective-permute-done.28
  164.8 4.2 collective-permute-done.30
  178.3 4.2 collective-permute-done.34
  185.9 4.2 collective-permute-done.36
  191.7 4.3 collective-permute-start.39
  198.0 46.9 %all-reduce.10 = (f32[]{:T(128)}, f32[]{:T(128)}) all-reduce(f32[]{:T(128)} %get-tuple-element.13, f32[]{:T(128)} %get-tuple-element.12), channel_id=1, replica_groups=mesh['gx'=2,'gy'=4,'gz'=4] {'gx','gy','gz'}, use_global_device_ids=true, to_apply=%region_3.4 | all-reduce | flops 2 | bytes 16 | tf_op jit(solution)/shard_map/psum | solution.py:78
  246.3 4.4 collective-permute-start.41
  252.2 4.2 collective-permute-done.40
  256.4 3.8 collective-permute-start.43
  261.7 4.2 collective-permute-done.42
  272.1 13.9 %reshape.82 = f32[3,4,2,8,2,64,2]{6,5,4,3,2,1,0:T(8,128)} reshape(f32[3,8,16,128]{3,2,1,0:T(8,128)S(1)} %fusion.103) | data formatting | bytes 393216 | tf_op jit(solution)/shard_map/reshape | solution.py:54
  286.0 5.5 reduce_sum.94
  291.5 11.0 %all-gather.1 = f32[12,4,8,64]{3,2,1,0:T(8,128)S(1)} all-gather(f32[3,4,8,64]{3,2,1,0:T(8,128)S(1)} %reduce_sum.94), channel_id=3, replica_groups=mesh['gx'=2,'gy'=4,'gz'=4] {'gz'}, dimensions={0}, use_global_device_ids=true | all-gather | bytes 122880 | tf_op jit(solution)/shard_map/all_gather | solution.py:103
  306.0 4.2 collective-permute-done.46
  314.3 4.2 collective-permute-done.48
  322.1 4.2 collective-permute-done.50
  329.7 4.2 collective-permute-done.52
  337.5 4.2 collective-permute-done.54
  345.1 4.2 collective-permute-done.56
  356.2 4.2 collective-permute-done.58
  363.7 4.2 collective-permute-done.60
  374.8 42.8 %psum.44 = f32[]{:T(128)} all-reduce(f32[]{:T(128)} %get-tuple-element.24), channel_id=1, replica_groups=mesh['gx'=2,'gy'=4,'gz'=4] {'gx','gy','gz'}, use_global_device_ids=true, to_apply=%region_8.9 | all-reduce | flops 1 | bytes 8 | tf_op jit(solution)/shard_map/psum | solution.py:78
  418.9 4.4 collective-permute-start.65
  424.8 4.2 collective-permute-done.64
  429.1 3.8 collective-permute-start.67
  434.3 4.2 collective-permute-done.66
  445.3 43.7 %psum.45 = f32[]{:T(128)} all-reduce(f32[]{:T(128)} %get-tuple-element.22), channel_id=1, replica_groups=mesh['gx'=2,'gy'=4,'gz'=4] {'gx','gy','gz'}, use_global_device_ids=true, to_apply=%region_10.11 | all-reduce | flops 1 | bytes 8 | tf_op jit(solution)/shard_map/psum | solution.py:122
  490.4 4.4 collective-permute-start.71
  496.3 4.2 collective-permute-done.70
  505.3 4.1 collective-permute-done.72
  515.6 13.9 %reshape.88 = f32[3,4,2,8,2,64,2]{6,5,4,3,2,1,0:T(8,128)} reshape(f32[3,8,16,128]{3,2,1,0:T(8,128)S(1)} %fusion.44) | data formatting | bytes 393216 | tf_op jit(solution)/shard_map/reshape | solution.py:54
  529.5 5.5 reduce_sum.97
  535.0 11.0 %all-gather.2 = f32[12,4,8,64]{3,2,1,0:T(8,128)S(1)} all-gather(f32[3,4,8,64]{3,2,1,0:T(8,128)S(1)} %reduce_sum.97), channel_id=4, replica_groups=mesh['gx'=2,'gy'=4,'gz'=4] {'gz'}, dimensions={0}, use_global_device_ids=true | all-gather | bytes 122880 | tf_op jit(solution)/shard_map/all_gather | solution.py:103
  549.5 4.2 collective-permute-done.76
  557.8 4.2 collective-permute-done.78
  565.6 4.2 collective-permute-done.80
  573.8 4.2 collective-permute-done.82
  581.6 4.2 collective-permute-done.84
  589.3 4.2 collective-permute-done.86
  598.3 4.2 collective-permute-done.88
  605.9 4.2 collective-permute-done.90
  617.9 42.8 %psum.46 = f32[]{:T(128)} all-reduce(f32[]{:T(128)} %get-tuple-element.18), channel_id=1, replica_groups=mesh['gx'=2,'gy'=4,'gz'=4] {'gx','gy','gz'}, use_global_device_ids=true, to_apply=%region_13.14 | all-reduce | flops 1 | bytes 8 | tf_op jit(solution)/shard_map/psum | solution.py:78
  662.0 4.4 collective-permute-start.95
  667.9 4.2 collective-permute-done.94
  677.4 4.2 collective-permute-done.96
  688.5 43.7 %psum.47 = f32[]{:T(128)} all-reduce(f32[]{:T(128)} %get-tuple-element.16), channel_id=1, replica_groups=mesh['gx'=2,'gy'=4,'gz'=4] {'gx','gy','gz'}, use_global_device_ids=true, to_apply=%region_15.16 | all-reduce | flops 1 | bytes 8 | tf_op jit(solution)/shard_map/psum | solution.py:122
  (301 shorter events, 196.0 us)
Async XLA Ops:
  1.3 15.3 %collective-permute-start.1 = (f32[1,16,128]{2,1,0:T(8,128)S(1)}, f32[1,16,128]{2,1,0:T(8,128)S(1)}, u32[]{:S(2)}, u32[]{:S(2)}) collective-permute-start(f32[1,16,128]{2,1,0:T(8,128)S(1)} %get-tuple-element.143), channel_id=1, source_target_pairs={{0,16},{1,17},{2,18},{3,19},{4,20},{5,21},{6,22},{7,23},{8,24},{9,... | collective-permute-start | bytes 24584 | tf_op jit(solution)/shard_map/ppermute | solution.py:20
  6.3 10.5 %collective-permute-start = (f32[1,16,128]{2,1,0:T(8,128)S(1)}, f32[1,16,128]{2,1,0:T(8,128)S(1)}, u32[]{:S(2)}, u32[]{:S(2)}) collective-permute-start(f32[1,16,128]{2,1,0:T(8,128)S(1)} %get-tuple-element.144), channel_id=1, source_target_pairs={{16,0},{17,1},{18,2},{19,3},{20,4},{21,5},{22,6},{23,7},{24,8},{25... | collective-permute-start | bytes 24584 | tf_op jit(solution)/shard_map/ppermute | solution.py:21
  16.8 12.1 %collective-permute-start.3 = (f32[10,1,128]{2,1,0:T(1,128)S(1)}, f32[10,1,128]{2,1,0:T(1,128)S(1)}, u32[]{:S(2)}, u32[]{:S(2)}) collective-permute-start(f32[10,1,128]{2,1,0:T(1,128)S(1)} %get-tuple-element.141), channel_id=1, source_target_pairs={{0,4},{4,8},{8,12},{1,5},{5,9},{9,13},{2,6},{6,10},{10,14},{3,7},{... | collective-permute-start | bytes 15368 | tf_op jit(solution)/shard_map/ppermute | solution.py:20
  20.3 8.7 %collective-permute-start.2 = (f32[10,1,128]{2,1,0:T(1,128)S(1)}, f32[10,1,128]{2,1,0:T(1,128)S(1)}, u32[]{:S(2)}, u32[]{:S(2)}) collective-permute-start(f32[10,1,128]{2,1,0:T(1,128)S(1)} %get-tuple-element.142), channel_id=1, source_target_pairs={{4,0},{8,4},{12,8},{5,1},{9,5},{13,9},{6,2},{10,6},{14,10},{7,3},{... | collective-permute-start | bytes 15368 | tf_op jit(solution)/shard_map/ppermute | solution.py:21
  29.1 9.4 %collective-permute-start.5 = (f32[10,18,1]{2,1,0:T(8,128)S(1)}, f32[10,18,1]{2,1,0:T(8,128)S(1)}, u32[]{:S(2)}, u32[]{:S(2)}) collective-permute-start(f32[10,18,1]{2,1,0:T(8,128)S(1)} %get-tuple-element.121), channel_id=1, source_target_pairs={{0,1},{1,2},{2,3},{4,5},{5,6},{6,7},{8,9},{9,10},{10,11},{12,13},{... | collective-permute-start | bytes 2168 | tf_op jit(solution)/shard_map/ppermute | solution.py:20
  31.3 7.2 collective-permute-start.4
  32.6 11.9 %collective-permute-start.13 = (f32[1,8,256]{2,1,0:T(8,128)S(1)}, f32[1,8,256]{2,1,0:T(8,128)S(1)}, u32[]{:S(2)}, u32[]{:S(2)}) collective-permute-start(f32[1,8,256]{2,1,0:T(8,128)S(1)} %get-tuple-element.147), channel_id=1, source_target_pairs={{0,16},{1,17},{2,18},{3,19},{4,20},{5,21},{6,22},{7,23},{8,24},{9,... | collective-permute-start | bytes 24584 | tf_op jit(solution)/shard_map/ppermute | solution.py:20
  37.2 7.4 %collective-permute-start.12 = (f32[1,8,256]{2,1,0:T(8,128)S(1)}, f32[1,8,256]{2,1,0:T(8,128)S(1)}, u32[]{:S(2)}, u32[]{:S(2)}) collective-permute-start(f32[1,8,256]{2,1,0:T(8,128)S(1)} %get-tuple-element.148), channel_id=1, source_target_pairs={{16,0},{17,1},{18,2},{19,3},{20,4},{21,5},{22,6},{23,7},{24,8},{25... | collective-permute-start | bytes 24584 | tf_op jit(solution)/shard_map/ppermute | solution.py:21
  38.7 11.7 %collective-permute-start.7 = (f32[3,1,16,128]{3,2,1,0:T(8,128)S(1)}, f32[3,1,16,128]{3,2,1,0:T(8,128)S(1)}, u32[]{:S(2)}, u32[]{:S(2)}) collective-permute-start(f32[3,1,16,128]{3,2,1,0:T(8,128)S(1)} %get-tuple-element.101), channel_id=1, source_target_pairs={{0,16},{1,17},{2,18},{3,19},{4,20},{5,21},{6,22},{7,23},{8,24},{9,... | collective-permute-start | bytes 73736 | tf_op jit(solution)/shard_map/ppermute | solution.py:20
  43.3 7.2 collective-permute-start.6
  44.6 11.8 %collective-permute-start.15 = (f32[6,1,256]{2,1,0:T(1,128)S(1)}, f32[6,1,256]{2,1,0:T(1,128)S(1)}, u32[]{:S(2)}, u32[]{:S(2)}) collective-permute-start(f32[6,1,256]{2,1,0:T(1,128)S(1)} %get-tuple-element.145), channel_id=1, source_target_pairs={{0,4},{4,8},{8,12},{1,5},{5,9},{9,13},{2,6},{6,10},{10,14},{3,7},{... | collective-permute-start | bytes 18440 | tf_op jit(solution)/shard_map/ppermute | solution.py:20
  49.2 7.2 collective-permute-start.14
  50.5 6.0 collective-permute-start.9
  55.1 5.6 collective-permute-start.8
  60.9 4.5 collective-permute-start.10
  98.5 6.1 collective-permute-start.17
  103.1 5.7 collective-permute-start.16
  108.8 4.9 collective-permute-start.19
  112.3 5.7 collective-permute-start.18
  120.1 5.7 collective-permute-start.20
  125.8 4.9 collective-permute-start.23
  129.3 5.7 collective-permute-start.22
  137.0 5.7 collective-permute-start.24
  144.7 5.7 collective-permute-start.26
  155.7 5.7 collective-permute-start.28
  163.4 5.6 collective-permute-start.30
  176.8 5.7 collective-permute-start.34
  184.5 5.6 collective-permute-start.36
  190.4 5.6 collective-permute-start.38
  191.7 5.4 collective-permute-start.39
  246.3 5.9 collective-permute-start.41
  250.7 5.7 collective-permute-start.40
  256.4 5.3 collective-permute-start.43
  260.3 5.6 collective-permute-start.42
  266.1 4.4 collective-permute-start.44
  304.5 5.7 collective-permute-start.46
  312.8 5.7 collective-permute-start.48
  320.6 5.7 collective-permute-start.50
  328.3 5.7 collective-permute-start.52
  336.0 5.7 collective-permute-start.54
  343.7 5.7 collective-permute-start.56
  354.7 5.7 collective-permute-start.58
  362.3 5.6 collective-permute-start.60
  368.2 4.4 collective-permute-start.62
  418.9 5.9 collective-permute-start.65
  423.3 5.7 collective-permute-start.64
  429.1 5.3 collective-permute-start.67
  432.9 5.6 collective-permute-start.66
  490.4 5.9 collective-permute-start.71
  494.8 5.7 collective-permute-start.70
  500.5 4.8 collective-permute-start.73
  503.8 5.6 collective-permute-start.72
  548.0 5.7 collective-permute-start.76
  556.3 5.7 collective-permute-start.78
  564.1 5.7 collective-permute-start.80
  572.4 5.7 collective-permute-start.82
  580.1 5.7 collective-permute-start.84
  587.8 5.7 collective-permute-start.86
  596.8 5.7 collective-permute-start.88
  604.5 5.6 collective-permute-start.90
  662.0 5.9 collective-permute-start.95
  666.4 5.7 collective-permute-start.94
  672.1 5.3 collective-permute-start.97
  676.0 5.6 collective-permute-start.96
  (40 other events, 331.3 us)
